TPU v7x, 32 devices: a whole 2x2x4 slice. The times are simulated.
32 devices in a mesh: ep: 8 (over y, x, core), tp: 4 (over z).
Axes of the slice: x: 2, y: 2, z: 4, core: 2. Of those that a mesh axis runs over, the one named last changes fastest.
Arguments:
- tokens: bfloat16 [256, 4096], P('ep', 'tp'), may hold values from -6 to 6
- norm_gains: float32 [2, 4096], replicated, may hold values from 0.1 to 1.9
- router: bfloat16 [2, 4096, 16], replicated, as said below
- w_gate: bfloat16 [2, 16, 4096, 768], P(None, 'ep', None, 'tp'), may hold values from -0.09375 to 0.09375
- w_up: bfloat16 [2, 16, 4096, 768], P(None, 'ep', None, 'tp'), may hold values from -0.09375 to 0.09375
- w_down: bfloat16 [2, 16, 768, 4096], P(None, 'ep', 'tp'), may hold values from -0.21875 to 0.21875
- expert_ids: int32 [2, 256, 8], P(None, 'ep'), may hold values from 0 to 15, all different within a row; in each aligned block of 32 rows (0 to 31, 32 to 63, ...) at most 32 rows name the same one
Outputs:
- hidden_out: bfloat16 [256, 4096], P('ep', 'tp')
Inputs may be any that keep to these rules, and one draw needn't show every extreme that they name: `expert_ids`: each entry names an expert of 0 to 15; the 8 entries of a token differ; among the 32 tokens of one ep index in one layer no expert is named more than 32 times, and in some such blocks one is named exactly 32 times. `router`: entries of order 2 / sqrt(4096); all columns of a layer may share a common added vector with entries of order 50 / sqrt(4096).
All inputs are finite; a program needn't handle non-finite values.
Results may differ from a plain program's by a relative error of at most 0.02.
Values may be sent and summed in bfloat16 or wider, within the bound.
A program may use at most 64 MiB of HBM per device.

v0:
```python
import jax
import jax.numpy as jnp
from jax import lax
from jax.sharding import PartitionSpec as P

TOP = 8
LAYERS = 2


norm_eps = 1e-06


def body(tokens, norm_gains, router, w_gate, w_up, w_down, expert_ids):
    n_tp = lax.axis_size("tp")
    n_ep = lax.axis_size("ep")
    local_width = tokens.shape[1]
    full_width = local_width * n_tp
    rows_dev = tokens.shape[0]
    local_exp = w_gate.shape[1]
    experts = local_exp * n_ep
    capacity = 2 * rows_dev * TOP // experts
    current = tokens
    for layer_idx in range(LAYERS):
        gain = norm_gains[layer_idx]
        weight = router[layer_idx]
        ids = expert_ids[layer_idx]
        normed = None
        whole = lax.all_gather(current, "tp", axis=1, tiled=True)
        wide_rows = whole.astype(jnp.float32)
        square_sum = jnp.sum(wide_rows * wide_rows, axis=1)
        scaled = (wide_rows * gain[None, :]).astype(jnp.bfloat16)
        raw_logits = jnp.dot(scaled, weight, preferred_element_type=jnp.float32)
        inverse = lax.rsqrt(square_sum / full_width + norm_eps)
        normed = (scaled.astype(jnp.float32) * inverse[:, None]).astype(jnp.bfloat16)
        logits = raw_logits * inverse[:, None]
        choose = ids[:, :, None] == lax.iota(jnp.int32, experts)[None, None, :]
        picked = jnp.sum(jnp.where(choose, logits[:, None, :], 0.0), axis=-1)
        gate_probs = jax.nn.softmax(picked, axis=-1)
        onehot = choose.reshape(rows_dev * TOP, experts).astype(jnp.int32)
        earlier = jnp.cumsum(onehot, axis=0) - onehot
        slot_index = jnp.sum(earlier * onehot, axis=1).reshape(rows_dev, TOP)
        slot_key = ids * capacity + slot_index
        slot_hits = slot_key[None, :, :] == lax.iota(jnp.int32, experts * capacity)[:, None, None]
        route_matrix = jnp.any(slot_hits, axis=-1).astype(jnp.bfloat16)
        combine_matrix = jnp.sum(jnp.where(slot_hits, gate_probs[None, :, :], 0.0), axis=-1).T
        outgoing = jnp.dot(route_matrix, normed, preferred_element_type=jnp.float32).astype(
            jnp.bfloat16
        )
        outgoing = outgoing.reshape(n_ep, local_exp * capacity, full_width)
        incoming = lax.all_to_all(outgoing, "ep", split_axis=0, concat_axis=0, tiled=True)
        arrived = incoming.reshape(n_ep, local_exp, capacity, full_width).transpose(1, 0, 2, 3)
        arrived = arrived.reshape(local_exp, n_ep * capacity, full_width)
        gate_proj = jnp.einsum(
            "erd,edf->erf", arrived, w_gate[layer_idx], preferred_element_type=jnp.float32
        )
        up_proj = jnp.einsum(
            "erd,edf->erf", arrived, w_up[layer_idx], preferred_element_type=jnp.float32
        )
        inner = (jax.nn.silu(gate_proj) * up_proj).astype(jnp.bfloat16)
        down_local = w_down[layer_idx]

        def project():
            down_piece = lax.slice_in_dim(down_local, 0, local_width * lax.axis_size("tp"), axis=2)
            return jnp.einsum("erf,efd->der", inner, down_piece, preferred_element_type=jnp.float32)

        summed = lax.psum_scatter(
            project().astype(jnp.bfloat16), "tp", scatter_dimension=0, tiled=True
        ).astype(jnp.float32)
        out_rows = summed.astype(jnp.bfloat16).reshape(local_width, local_exp, n_ep, capacity)
        out_rows = out_rows.transpose(2, 1, 3, 0).reshape(n_ep, local_exp * capacity, local_width)
        returned = lax.all_to_all(out_rows, "ep", split_axis=0, concat_axis=0, tiled=True)
        returned = returned.reshape(experts * capacity, local_width).astype(jnp.float32)
        moe_out = jnp.dot(combine_matrix, returned, precision=lax.Precision.HIGHEST)
        current = (current.astype(jnp.float32) + moe_out).astype(jnp.bfloat16)
    return current


def solution(mesh):
    in_specs = (
        P("ep", "tp"),
        P(),
        P(),
        P(None, "ep", None, "tp"),
        P(None, "ep", None, "tp"),
        P(None, "ep", "tp", None),
        P(None, "ep", None),
    )
    out_specs = P("ep", "tp")
    return jax.shard_map(body, mesh=mesh, in_specs=in_specs, out_specs=out_specs, check_vma=False)
```

profile of v0, /device:TPU:0, one launch (start us, length us, event | category | flops | bytes accessed | tf_op | source)
XLA Modules:
  0.0 376.5 jit_solution(15348728780867839647)
XLA Ops:
  6.5 0.0 reduce-scatter.3.cloned.1.call-start
  6.5 0.7 fusion.79
  7.2 0.1 copy.38
  7.3 0.1 eq.102
  7.4 0.1 eq.98
  7.5 0.6 reduce-window.14
  8.1 0.2 slice_reduce_fusion.1
  8.3 0.1 fusion.69
  8.4 0.1 reshape.147
  8.5 0.2 fusion.41
  8.8 0.9 fusion.78
  9.6 15.7 %all_gather.6 = bf16[32,4096]{1,0:T(8,128)(2,1)S(1)} all-gather(bf16[32,1024]{1,0:T(8,128)(2,1)} %param.7), channel_id=1, replica_groups=mesh['ep'=8,'tp'=4] {'tp'}, dimensions={1}, use_global_device_ids=true | all-gather | bytes 327680 | tf_op jit(solution)/shard_map/all_gather | solution.py:28
  25.4 0.2 fusion.37
  25.5 1.3 convolution_convert_fusion.3
  26.9 0.0 slice-start
  26.9 52.8 %all_to_all.20 = bf16[8,64,4096]{2,1,0:T(8,128)(2,1)S(1)} all-to-all(bf16[8,64,4096]{2,1,0:T(8,128)(2,1)S(1)} %bitcast.120), channel_id=1, replica_groups=mesh['ep'=8,'tp'=4] {'ep'}, dimensions={0} | all-to-all | bytes 8388608 | tf_op jit(solution)/shard_map/all_to_all | solution.py:50
  79.7 0.5 copy.30
  80.2 0.0 copy-start
  80.2 2.0 copy-done
  82.2 0.0 slice-done
  82.2 0.0 slice-done.1
  82.2 1.5 fusion.10
  83.7 8.8 %fusion = bf16[4096,2,256]{0,2,1:T(8,128)(2,1)} fusion(bf16[2,2,192,4096]{3,2,1,0:T(8,128)(2,1)} %param.12, bf16[2,256,4096]{2,1,0:T(8,128)(2,1)} %bitcast.125, bf16[2,2,4096,192]{2,3,1,0:T(8,128)(2,1)} %param.11, f32[2,256,192]{1,2,0:T(8,128)S(1)} %fusion.10), kind=kOutput, calls=%fused_computation.4 | convolution fusion | flops 1613299712 | bytes 15073280 | tf_op jit(solution)/shard_map/erf,efd->der/dot_general | solution.py:64
  92.5 0.0 reduce-scatter.3.cloned.1.call-update
  92.5 0.1 copy.39
  92.6 0.1 eq.118
  92.7 0.1 eq.114
  92.8 0.6 reduce-window.16
  93.4 0.2 slice_reduce_fusion
  93.6 0.1 fusion.66
  93.7 0.1 reshape.155
  93.8 0.0 copy-done.3
  93.8 0.2 convolution_multiply_fusion.1
  94.0 75.2 %reduce-scatter.3.cloned.1.call-done = bf16[1024,2,256]{0,2,1:T(8,128)(2,1)} async-done(((bf16[4096,2,256]{0,2,1:T(8,128)(2,1)}), bf16[1024,2,256]{0,2,1:T(8,128)(2,1)}) %reduce-scatter.3.cloned.1.call-update) | async-done | bytes 1048592 | tf_op jit(solution)/shard_map/reduce_scatter | solution.py:66
  169.2 2.3 copy.31
  171.5 3.7 all-to-all-start.1
  175.2 0.0 reduce-scatter.5.cloned.1.call-start
  175.3 0.1 copy.29
  175.4 0.2 fusion.40
  175.7 0.2 select_reduce_fusion.1
  175.9 14.9 %all-to-all-done.1 = bf16[8,64,1024]{2,1,0:T(8,128)(2,1)S(1)} async-done(((bf16[8,64,1024]{2,1,0:T(8,128)(2,1)}), bf16[8,64,1024]{2,1,0:T(8,128)(2,1)S(1)}, u32[]{:S(2)}, u32[]{:S(2)}) %all-to-all-start.1) | async-done | bytes 1048608 | tf_op jit(solution)/shard_map/all_to_all | solution.py:71
  190.8 0.0 copy-done.2
  190.8 0.6 fusion.30
  191.4 14.0 %all_gather.7 = bf16[32,4096]{1,0:T(8,128)(2,1)S(1)} all-gather(bf16[32,1024]{1,0:T(8,128)(2,1)S(1)} %fusion.30), channel_id=1, replica_groups=mesh['ep'=8,'tp'=4] {'tp'}, dimensions={1}, use_global_device_ids=true | all-gather | bytes 327680 | tf_op jit(solution)/shard_map/all_gather | solution.py:28
  205.4 0.2 fusion.39
  205.5 1.3 convolution_convert_fusion.1
  206.9 0.0 slice-start.2
  206.9 51.8 %all_to_all.21 = bf16[8,64,4096]{2,1,0:T(8,128)(2,1)S(1)} all-to-all(bf16[8,64,4096]{2,1,0:T(8,128)(2,1)S(1)} %bitcast.122), channel_id=1, replica_groups=mesh['ep'=8,'tp'=4] {'ep'}, dimensions={0} | all-to-all | bytes 8388608 | tf_op jit(solution)/shard_map/all_to_all | solution.py:50
  258.7 0.5 copy.36
  259.1 0.0 copy-start.1
  259.2 2.0 copy-done.1
  261.1 0.0 slice-done.2
  261.1 0.0 slice-done.3
  261.1 1.5 fusion.5
  262.7 8.8 %fusion.1 = bf16[4096,2,256]{0,2,1:T(8,128)(2,1)} fusion(bf16[2,2,192,4096]{3,2,1,0:T(8,128)(2,1)} %param.12, bf16[2,256,4096]{2,1,0:T(8,128)(2,1)} %bitcast.127, bf16[2,2,4096,192]{2,3,1,0:T(8,128)(2,1)} %param.11, f32[2,256,192]{1,2,0:T(8,128)S(1)} %fusion.5), kind=kOutput, calls=%fused_computation.5 | convolution fusion | flops 1613299712 | bytes 15073280 | tf_op jit(solution)/shard_map/erf,efd->der/dot_general | solution.py:64
  271.5 0.0 reduce-scatter.5.cloned.1.call-update
  271.5 75.4 %reduce-scatter.5.cloned.1.call-done = bf16[1024,2,256]{0,2,1:T(8,128)(2,1)} async-done(((bf16[4096,2,256]{0,2,1:T(8,128)(2,1)}), bf16[1024,2,256]{0,2,1:T(8,128)(2,1)}) %reduce-scatter.5.cloned.1.call-update) | async-done | bytes 1048592 | tf_op jit(solution)/shard_map/reduce_scatter | solution.py:66
  346.9 2.3 copy.37
  349.2 3.7 all-to-all-start.3
  352.9 0.2 convolution_multiply_fusion
  353.2 0.1 copy.35
  353.2 0.2 select_reduce_fusion
  353.5 15.0 %all-to-all-done.3 = bf16[8,64,1024]{2,1,0:T(8,128)(2,1)S(1)} async-done(((bf16[8,64,1024]{2,1,0:T(8,128)(2,1)}), bf16[8,64,1024]{2,1,0:T(8,128)(2,1)S(1)}, u32[]{:S(2)}, u32[]{:S(2)}) %all-to-all-start.3) | async-done | bytes 1048608 | tf_op jit(solution)/shard_map/all_to_all | solution.py:71
  368.4 1.2 fusion.31
  (24 shorter events, 0.3 us)
Async XLA Ops:
  6.5 162.7 %reduce-scatter.3.cloned.1.call-start = ((), (), s32[]{:S(2)}) async-start(), calls=%async_computation.6 | async-start | bytes 5242880 | tf_op jit(solution)/shard_map/reduce_scatter | solution.py:66
  26.9 55.3 %slice-start = ((s8[6291456]{0:T(1024)(128)(4,1)}), s8[4194304]{0:T(1024)(128)(4,1)S(1)}, s32[]{:S(2)}) async-start(s8[6291456]{0:T(1024)(128)(4,1)} %bitcast.136), calls=%async_computation.8 | async-start | bytes 8388608
  79.7 2.5 slice-start.1
  80.2 2.0 copy-start
  92.5 1.3 copy-start.3
  92.5 98.3 %copy-start.2 = (bf16[32,1024]{1,0:T(8,128)(2,1)S(1)}, bf16[32,1024]{1,0:T(8,128)(2,1)}, u32[]{:S(2)}) copy-start(bf16[32,1024]{1,0:T(8,128)(2,1)} %param.7) | copy-start | bytes 196612
  171.5 19.2 %all-to-all-start.1 = ((bf16[8,64,1024]{2,1,0:T(8,128)(2,1)}), bf16[8,64,1024]{2,1,0:T(8,128)(2,1)S(1)}, u32[]{:S(2)}, u32[]{:S(2)}) async-start(bf16[8,64,1024]{2,1,0:T(8,128)(2,1)} %bitcast.16), calls=%async_computation.2 | async-start | bytes 2097152 | tf_op jit(solution)/shard_map/all_to_all | solution.py:71
  175.2 171.7 %reduce-scatter.5.cloned.1.call-start = ((), (), s32[]{:S(2)}) async-start(), calls=%async_computation.7 | async-start | bytes 5242880 | tf_op jit(solution)/shard_map/reduce_scatter | solution.py:66
  206.9 54.3 %slice-start.2 = ((s8[6291456]{0:T(1024)(128)(4,1)}), s8[4194304]{0:T(1024)(128)(4,1)S(1)}, s32[]{:S(2)}) async-start(s8[6291456]{0:T(1024)(128)(4,1)} %bitcast.138), calls=%async_computation.10 | async-start | bytes 8388608
  258.7 2.5 slice-start.3
  259.1 2.0 copy-start.1
  349.2 19.2 %all-to-all-start.3 = ((bf16[8,64,1024]{2,1,0:T(8,128)(2,1)}), bf16[8,64,1024]{2,1,0:T(8,128)(2,1)S(1)}, u32[]{:S(2)}, u32[]{:S(2)}) async-start(bf16[8,64,1024]{2,1,0:T(8,128)(2,1)} %bitcast.34), calls=%async_computation.5 | async-start | bytes 2097152 | tf_op jit(solution)/shard_map/all_to_all | solution.py:71
Sparse Core Ops, SparseCore 0:
  92.7 76.5 reduce-scatter.2
  271.6 75.2 reduce-scatter.4
where the time goes:
time: 377 us
  waiting for transfers between devices  181 us (48%)
  blocking collectives  134 us (36%)
  matrix products  25.5 us (7%)
  between operations  13.6 us (4%)
  local copies, waits for them, and re-layouts  12.3 us (3%)
  starting transfers between devices  7.35 us (2%)
    reduce_scatter x2, waiting for transfers between devices, body(): lax.psum_scatter(project().astype(jnp.bfloat16), 'tp', scatter_dimension=...  151 us
    all_to_all x2, blocking collectives, body(): lax.all_to_all(outgoing, 'ep', split_axis=0, concat_axis=0, tiled=True)  105 us
    all_to_all x2, waiting for transfers between devices, body(): lax.all_to_all(out_rows, 'ep', split_axis=0, concat_axis=0, tiled=True)  29.8 us
    all_gather x2, blocking collectives, body(): whole = lax.all_gather(current, 'tp', axis=1, tiled=True)  29.7 us
    dot_general x2, matrix products, project(): jnp.einsum('erf,efd->der', inner, down_piece, preferred_element_type=jnp....  17.6 us
  transfers between devices with their start and end apart: 4, of which 4 were waited for; matrix products, arithmetic and copies ran while one was open for 1% of the time, Pallas kernels for 0%

commit v1 on v0

v1 whole, which is shorter than its diff:
```python
import functools

import jax
import jax.numpy as jnp
from jax import lax
from jax.experimental import pallas as pl
from jax.experimental.pallas import tpu as pltpu
from jax.sharding import PartitionSpec as P

MESH = pl.DeviceIdType.MESH
BF16, F32 = jnp.bfloat16, jnp.float32
CORES = 2
LANES = 128

norm_eps = 1e-06


def kernel(
    n_ep, n_tp, layers,
    tokens, gains, router, w_gate, w_up, w_down, ids,
    out,
    x, mask, w_in, wd, acc, sacc, inner, own, pair_out, pair_in, plane_out, plane_in,
    line_out, line_in,
    w_sem, mask_send, mask_recv, x_send, x_recv, pair_send, pair_recv, plane_send, plane_recv,
    line_send, line_recv,
):
    rows, width = tokens.shape
    chips = n_ep // CORES
    half = chips * rows
    local_exp, hidden_units = w_gate.shape[1:3]
    experts, top = router.shape[1], ids.shape[1]
    held = local_exp * hidden_units
    me, z = lax.axis_index("ep"), lax.axis_index("tp")
    q, c = me // CORES, lax.rem(me, CORES)
    sibling = (q * CORES + 1 - c, z)

    def chip(k):
        return lax.rem(q + k, chips)

    def plane_dev(k):
        return (chip(k) * CORES + c, z)

    def line_dev(k):
        return (me, lax.rem(z + k, n_tp))

    def at_rows(index, base=0):
        return pl.ds(pl.multiple_of(base + index * rows, rows), rows)

    def columns(dz):
        return pl.ds(pl.multiple_of(lax.rem(z + dz, n_tp) * width, width), width)

    def weight_copies(l):
        pairs = [(router.at[l], w_in.at[l, pl.ds(2 * held, experts), :])]
        for i, source in enumerate((w_gate, w_up)):
            for e in range(local_exp):
                place = pl.ds(i * held + e * hidden_units, hidden_units)
                pairs.append((source.at[l, e], w_in.at[l, place, :]))
        pairs.append((w_down.at[l], wd.at[l]))
        return [
            pltpu.make_async_copy(src, dst, w_sem.at[l, i]) for i, (src, dst) in enumerate(pairs)
        ]

    for l in range(layers):
        for copy in weight_copies(l):
            copy.start()

    barrier = pltpu.get_barrier_semaphore()
    for k in range(1, n_ep):
        pl.semaphore_signal(
            barrier, inc=1, device_id=(lax.rem(me + k, n_ep), z), device_id_type=MESH
        )
    for k in range(1, n_tp):
        pl.semaphore_signal(barrier, inc=1, device_id=line_dev(k), device_id_type=MESH)

    x[0, 0, at_rows(q), :] = tokens[...]
    lane = lax.broadcasted_iota(jnp.int32, (rows, mask.shape[2]), 1)
    for l in range(layers):
        chosen = ids[l].T
        hit = chosen[:, 0:1] == lane
        for k in range(1, top):
            hit = hit | (chosen[:, k : k + 1] == lane)
        mask[l, at_rows(q), :] = jnp.where(hit, 1.0, 0.0).astype(BF16)

    pl.semaphore_wait(barrier, n_ep - 1 + n_tp - 1)

    def remote(src, dst, send, recv, device):
        return pltpu.make_async_remote_copy(
            src_ref=src, dst_ref=dst, send_sem=send, recv_sem=recv,
            device_id=device, device_id_type=MESH,
        )

    mask_copies = []
    for k in range(1, n_ep):
        mask_copies.append(
            remote(
                mask.at[:, at_rows(q), :],
                mask.at[:, at_rows(q, (k % CORES) * half), :],
                mask_send.at[k], mask_recv.at[k],
                (lax.rem(me + k, n_ep), z),
            )
        )

    def layer(l, carry):
        sends = []

        def go(copy):
            copy.start()
            sends.append(copy)

        def to_line(k):
            there = (-k) % n_tp
            mine = x.at[l, 0, at_rows(q), :]
            return remote(
                mine, x.at[l, there, at_rows(q), :],
                x_send.at[l, 0, k, 0], x_recv.at[l, 0, there, q], line_dev(k),
            )

        def to_plane(dz, k):
            ref = x.at[l, dz, at_rows(q), :]
            return remote(
                ref, ref, x_send.at[l, 1, dz, k], x_recv.at[l, 0, dz, q], plane_dev(k)
            )

        def to_sibling(dz, k):
            return remote(
                x.at[l, dz, at_rows(chip(k)), :],
                x.at[l, dz, at_rows(chip(k), half), :],
                x_send.at[l, 2, dz, k], x_recv.at[l, 1, dz, chip(k)], sibling,
            )

        def arrive(parity, dz, k):
            ref = x.at[l, dz, at_rows(chip(k), parity * half), :]
            pltpu.make_async_remote_copy(
                src_ref=ref, dst_ref=ref, send_sem=x_send.at[l, 0, 0, 0],
                recv_sem=x_recv.at[l, parity, dz, chip(k)],
                device_id=sibling, device_id_type=MESH,
            ).wait_recv()

        order = sorted(range(n_tp), key=lambda k: min(k, n_tp - k))
        for k in range(1, n_tp):
            go(to_line(k))
        for k in range(1, chips):
            go(to_plane(0, k))
        go(to_sibling(0, 0))

        @pl.when(l == 0)
        def _():
            for copy in mask_copies:
                copy.start()

        for dz in order[1:]:
            arrive(0, dz, 0)
            for k in range(1, chips):
                go(to_plane(dz, k))
            go(to_sibling(dz, 0))

        for copy in weight_copies(l)[:-1]:
            copy.wait()
        for i, dz in enumerate(order):
            for k in range(1, chips):
                arrive(0, dz, k)
                go(to_sibling(dz, k))
            for k in range(chips):
                arrive(1, dz, k)
            block = x[l, dz].astype(F32)
            square = jnp.sum(block * block, axis=1, keepdims=True)
            scaled = (block * gains[pl.ds(l, 1), columns(dz)]).astype(BF16)
            sums = lax.dot_general(
                scaled, w_in[l, :, columns(dz)], (((1,), (1,)), ((), ())),
                preferred_element_type=F32,
            )
            if i == 0:
                sacc[...] = square
                acc[...] = sums
            else:
                sacc[...] += square
                acc[...] += sums

        @pl.when(l == 0)
        def _():
            for copy in mask_copies:
                copy.wait_recv()

        inverse = lax.rsqrt(sacc[...] / (width * n_tp) + norm_eps)
        logits = acc[:, 2 * held :] * inverse
        hit = mask[l][:, :experts].astype(F32) > 0.5
        logits = jnp.where(hit, logits, -jnp.inf)
        grown = jnp.exp(logits - jnp.max(logits, axis=1, keepdims=True))
        gates = grown / jnp.sum(grown, axis=1, keepdims=True)
        expert = lax.broadcasted_iota(jnp.int32, gates.shape, 1)
        unit = lax.broadcasted_iota(jnp.int32, (1, held), 1)
        weight = None
        for e in range(local_exp):
            gate = jnp.sum(
                jnp.where(expert == me * local_exp + e, gates, 0.0), axis=1, keepdims=True
            )
            weight = gate if e == 0 else jnp.where(unit < e * hidden_units, weight, gate)
        v = acc[:, :held] * inverse
        u = acc[:, held : 2 * held] * inverse
        inner[...] = (v / (1.0 + jnp.exp(-v)) * u * weight).astype(BF16)

        weight_copies(l)[-1].wait()

        def project(dz):
            total = jnp.dot(inner[...], wd[l, :, columns(dz)], preferred_element_type=F32)
            pair_out[dz] = total[half:].astype(BF16)
            own[dz] = total[:half]
            go(remote(
                pair_out.at[dz], pair_in.at[dz],
                pair_send.at[l, dz], pair_recv.at[l, dz], sibling,
            ))

        def landed(ref, send, recv):
            pltpu.make_async_remote_copy(
                src_ref=ref, dst_ref=ref, send_sem=send, recv_sem=recv,
                device_id=sibling, device_id_type=MESH,
            ).wait_recv()

        def spread(dz):
            landed(pair_in.at[dz], pair_send.at[l, dz], pair_recv.at[l, dz])
            total = own[dz] + pair_in[dz].astype(F32)
            own[dz] = total
            plane_out[dz] = total.astype(BF16)
            for k in range(1, chips):
                there = (-k) % chips
                go(remote(
                    plane_out.at[dz, at_rows(chip(k)), :], plane_in.at[l, dz, there],
                    plane_send.at[l, dz, k], plane_recv.at[l, dz, there], plane_dev(k),
                ))

        def gather(dz):
            total = own[dz, at_rows(q), :]
            for k in range(1, chips):
                landed(
                    plane_in.at[l, dz, k], plane_send.at[l, dz, k], plane_recv.at[l, dz, k]
                )
                total = total + plane_in[l, dz, k].astype(F32)
            return total

        back = order[::-1]
        for i, dz in enumerate(back):
            project(dz)
            if i > 0:
                spread(back[i - 1])
        spread(back[-1])
        moe = None
        for dz in back:
            moe = gather(dz)
            if dz != 0:
                there = (-dz) % n_tp
                line_out[l, dz] = moe.astype(BF16)
                go(remote(
                    line_out.at[l, dz], line_in.at[l, there],
                    line_send.at[l, dz], line_recv.at[l, there], line_dev(dz),
                ))
        for k in order[1:]:
            landed(line_in.at[l, k], line_send.at[l, k], line_recv.at[l, k])
            moe = moe + line_in[l, k].astype(F32)
        hidden = (x[l, 0, at_rows(q), :].astype(F32) + moe).astype(BF16)
        for copy in sends:
            copy.wait_send()
        out[...] = hidden

        @pl.when(l < layers - 1)
        def _():
            x[lax.rem(l + 1, layers), 0, at_rows(q), :] = hidden

        return carry

    lax.fori_loop(0, layers, layer, 0)
    for copy in mask_copies:
        copy.wait_send()


def body(tokens, norm_gains, router, w_gate, w_up, w_down, expert_ids):
    n_ep, n_tp = lax.axis_size("ep"), lax.axis_size("tp")
    layers, local_exp, full, hidden = w_gate.shape
    experts = router.shape[2]
    rows, width = tokens.shape
    held = local_exp * hidden
    chips = n_ep // CORES
    every, half = n_ep * rows, chips * rows
    vmem = pl.BlockSpec(memory_space=pltpu.VMEM)
    hbm = pl.BlockSpec(memory_space=pl.ANY)
    dma = pltpu.SemaphoreType.DMA
    lanes = -(-experts // LANES) * LANES
    return pl.pallas_call(
        functools.partial(kernel, n_ep, n_tp, layers),
        out_shape=jax.ShapeDtypeStruct((rows, width), BF16),
        in_specs=[vmem, vmem, vmem, hbm, hbm, hbm, vmem],
        out_specs=vmem,
        scratch_shapes=[
            pltpu.VMEM((layers, n_tp, every, width), BF16),
            pltpu.VMEM((layers, every, lanes), BF16),
            pltpu.VMEM((layers, 2 * held + experts, full), BF16),
            pltpu.VMEM((layers, held, full), BF16),
            pltpu.VMEM((every, 2 * held + experts), F32),
            pltpu.VMEM((every, 1), F32),
            pltpu.VMEM((every, held), BF16),
            pltpu.VMEM((n_tp, half, width), F32),
            pltpu.VMEM((n_tp, half, width), BF16),
            pltpu.VMEM((n_tp, half, width), BF16),
            pltpu.VMEM((n_tp, half, width), BF16),
            pltpu.VMEM((layers, n_tp, chips, rows, width), BF16),
            pltpu.VMEM((layers, n_tp, rows, width), BF16),
            pltpu.VMEM((layers, n_tp, rows, width), BF16),
            dma((layers, 2 + 2 * local_exp)),
            dma((n_ep,)),
            dma((n_ep,)),
            dma((layers, 3, n_tp, chips)),
            dma((layers, 2, n_tp, chips)),
            dma((layers, n_tp)),
            dma((layers, n_tp)),
            dma((layers, n_tp, chips)),
            dma((layers, n_tp, chips)),
            dma((layers, n_tp)),
            dma((layers, n_tp)),
        ],
        compiler_params=pltpu.CompilerParams(
            collective_id=0, has_side_effects=True, vmem_limit_bytes=67043328
        ),
    )(
        tokens, norm_gains, router.swapaxes(1, 2), w_gate.swapaxes(2, 3), w_up.swapaxes(2, 3),
        w_down.reshape(layers, held, full), expert_ids.swapaxes(1, 2),
    )


def solution(mesh):
    in_specs = (
        P("ep", "tp"),
        P(),
        P(),
        P(None, "ep", None, "tp"),
        P(None, "ep", None, "tp"),
        P(None, "ep", "tp", None),
        P(None, "ep", None),
    )
    return jax.shard_map(
        body, mesh=mesh, in_specs=in_specs, out_specs=P("ep", "tp"), check_vma=False
    )
```

time: 377 us -> 82.5 us (0.22)
  waiting for transfers between devices: 181 us -> 0 us
  blocking collectives: 134 us -> 0 us
  Pallas kernels: 0 us -> 80.9 us
  matrix products: 25.5 us -> 0 us
  between operations: 13.6 us -> 0.01 us
  local copies, waits for them, and re-layouts: 12.3 us -> 1.47 us
  starting transfers between devices: 7.35 us -> 0 us
    reduce_scatter x2 -> x0, waiting for transfers between devices: 151 us -> none  [body(): lax.psum_scatter(project().astype(jnp.bfloat16), 'tp', scatter_dimension=...]
    all_to_all x2 -> x0, blocking collectives: 105 us -> none  [body(): lax.all_to_all(outgoing, 'ep', split_axis=0, concat_axis=0, tiled=True)]
    pallas_call x0 -> x1, Pallas kernels: none -> 80.9 us  [body(): pl.pallas_call(functools.partial(kernel, n_ep, n_tp, layers), out_shape=j...]
    all_to_all x2 -> x0, waiting for transfers between devices: 29.8 us -> none  [body(): lax.all_to_all(out_rows, 'ep', split_axis=0, concat_axis=0, tiled=True)]
    all_gather x2 -> x0, blocking collectives: 29.7 us -> none  [body(): whole = lax.all_gather(current, 'tp', axis=1, tiled=True)]
    dot_general x10 -> x0, matrix products: 25.5 us -> none  [the longest x2 17.6 us: project(): jnp.einsum('erf,efd->der', inner, down_piece, preferred_element_type=jnp....]
    all_to_all x2 -> x0, starting transfers between devices: 7.32 us -> none  [body(): lax.all_to_all(out_rows, 'ep', split_axis=0, concat_axis=0, tiled=True)]
    reshape x6 -> x0, local copies, waits for them, and re-layouts: 5.75 us -> none  [the longest x2 4.61 us: body(): summed.astype(jnp.bfloat16).reshape(local_width, local_exp, n_ep, capacity)]
  transfers between devices with their start and end apart: 4 -> 0, of which waited for: 4 -> 0; matrix products, arithmetic and copies ran while one was open for 1% -> 0% of each run, Pallas kernels for 0% -> 0%
where the time goes in v1:
time: 82.5 us; the launch traced here: 82.4 us
  Pallas kernels  80.9 us (98%)
  local copies, waits for them, and re-layouts  1.47 us (2%)
    pallas_call x1, Pallas kernels, body(): pl.pallas_call(functools.partial(kernel, n_ep, n_tp, layers), out_shape=j...  80.9 us

profile of v1, /device:TPU:0, one launch (start us, length us, event | category | flops | bytes accessed | tf_op | source)
XLA Modules:
  0.0 82.4 jit_solution(17497698948267246523)
XLA Ops:
  0.0 80.9 %shard_map.73 = bf16[32,1024]{1,0:T(8,128)(2,1)} custom-call(bf16[32,1024]{1,0:T(8,128)(2,1)} %tokens.1, f32[2,4096]{1,0:T(2,128)} %gains.1, bf16[2,16,4096]{2,1,0:T(8,128)(2,1)} %bitcast.8, bf16[2,2,192,4096]{3,2,1,0:T(8,128)(2,1)} %bitcast.5, bf16[2,2,192,4096]{3,2,1,0:T(8,128)(2,1)} %bitcast.6, bf16[2,384,4096]{2,1,0:T(8,128)(2,1)} %bitcast.7, ...), custom_call_target="tpu_custom_call" | custom-call | tf_op jit(solution)/shard_map/pallas_call | solution.py:287
  80.9 1.5 %copy.9 = bf16[32,1024]{1,0:T(8,128)(2,1)} copy(bf16[32,1024]{1,0:T(8,128)(2,1)} %shard_map.73) | data formatting | bytes 131072

commit v2 on v1

--- a/solution.py
+++ b/solution.py
@@ -13,6 +13,15 @@
 LANES = 128
 
 norm_eps = 1e-06
+
+
+def flip(index, k):
+    bit = 1
+    while bit <= k:
+        if k & bit:
+            index = index + bit * (1 - 2 * lax.rem(index // bit, 2))
+        bit *= 2
+    return index
 
 
 def kernel(
@@ -34,20 +43,25 @@
     q, c = me // CORES, lax.rem(me, CORES)
     sibling = (q * CORES + 1 - c, z)
 
+    relay = chips == 4
+
     def chip(k):
-        return lax.rem(q + k, chips)
+        if relay and 0 < k < 3:
+            one, two = flip(q, k), flip(q, 3 - k)
+            return one + c * (two - one)
+        return flip(q, k)
 
     def plane_dev(k):
         return (chip(k) * CORES + c, z)
 
     def line_dev(k):
-        return (me, lax.rem(z + k, n_tp))
+        return (me, flip(z, k))
 
     def at_rows(index, base=0):
         return pl.ds(pl.multiple_of(base + index * rows, rows), rows)
 
     def columns(dz):
-        return pl.ds(pl.multiple_of(lax.rem(z + dz, n_tp) * width, width), width)
+        return pl.ds(pl.multiple_of(flip(z, dz) * width, width), width)
 
     def weight_copies(l):
         pairs = [(router.at[l], w_in.at[l, pl.ds(2 * held, experts), :])]
@@ -73,13 +87,14 @@
         pl.semaphore_signal(barrier, inc=1, device_id=line_dev(k), device_id_type=MESH)
 
     x[0, 0, at_rows(q), :] = tokens[...]
-    lane = lax.broadcasted_iota(jnp.int32, (rows, mask.shape[2]), 1)
+    lane = lax.broadcasted_iota(jnp.int32, (rows, mask.shape[1]), 1)
+    hit = None
     for l in range(layers):
-        chosen = ids[l].T
-        hit = chosen[:, 0:1] == lane
-        for k in range(1, top):
-            hit = hit | (chosen[:, k : k + 1] == lane)
-        mask[l, at_rows(q), :] = jnp.where(hit, 1.0, 0.0).astype(BF16)
+        chosen = ids[l].T + l * experts
+        for k in range(top):
+            named = chosen[:, k : k + 1] == lane
+            hit = named if hit is None else hit | named
+    mask[at_rows(q), :] = jnp.where(hit, 1.0, 0.0).astype(BF16)
 
     pl.semaphore_wait(barrier, n_ep - 1 + n_tp - 1)
 
@@ -93,8 +108,8 @@
     for k in range(1, n_ep):
         mask_copies.append(
             remote(
-                mask.at[:, at_rows(q), :],
-                mask.at[:, at_rows(q, (k % CORES) * half), :],
+                mask.at[at_rows(q), :],
+                mask.at[at_rows(q, (k % CORES) * half), :],
                 mask_send.at[k], mask_recv.at[k],
                 (lax.rem(me + k, n_ep), z),
             )
@@ -108,17 +123,22 @@
             sends.append(copy)
 
         def to_line(k):
-            there = (-k) % n_tp
             mine = x.at[l, 0, at_rows(q), :]
             return remote(
-                mine, x.at[l, there, at_rows(q), :],
-                x_send.at[l, 0, k, 0], x_recv.at[l, 0, there, q], line_dev(k),
+                mine, x.at[l, k, at_rows(q), :],
+                x_send.at[l, 0, k, 0], x_recv.at[l, 0, k, q], line_dev(k),
             )
 
         def to_plane(dz, k):
             ref = x.at[l, dz, at_rows(q), :]
             return remote(
                 ref, ref, x_send.at[l, 1, dz, k], x_recv.at[l, 0, dz, q], plane_dev(k)
+            )
+
+        def onward(dz):
+            ref = x.at[l, dz, at_rows(chip(1)), :]
+            return remote(
+                ref, ref, x_send.at[l, 1, dz, 3], x_recv.at[l, 0, dz, chip(1)], plane_dev(2)
             )
 
         def to_sibling(dz, k):
@@ -136,10 +156,10 @@
                 device_id=sibling, device_id_type=MESH,
             ).wait_recv()
 
-        order = sorted(range(n_tp), key=lambda k: min(k, n_tp - k))
+        near = range(1, 3 if relay else chips)
         for k in range(1, n_tp):
             go(to_line(k))
-        for k in range(1, chips):
+        for k in near:
             go(to_plane(0, k))
         go(to_sibling(0, 0))
 
@@ -148,20 +168,27 @@
             for copy in mask_copies:
                 copy.start()
 
-        for dz in order[1:]:
-            arrive(0, dz, 0)
-            for k in range(1, chips):
-                go(to_plane(dz, k))
-            go(to_sibling(dz, 0))
-
-        for copy in weight_copies(l)[:-1]:
-            copy.wait()
-        for i, dz in enumerate(order):
-            for k in range(1, chips):
+        def pass_on(dz):
+            if dz + 1 < n_tp:
+                arrive(0, dz + 1, 0)
+                for k in near:
+                    go(to_plane(dz + 1, k))
+                go(to_sibling(dz + 1, 0))
+            for k in near:
                 arrive(0, dz, k)
+                if relay and k == 1:
+                    go(onward(dz))
                 go(to_sibling(dz, k))
+
+        def complete(dz):
+            if relay:
+                arrive(0, dz, 3)
+                go(to_sibling(dz, 3))
             for k in range(chips):
                 arrive(1, dz, k)
+            if dz == 0:
+                for copy in weight_copies(l)[:-1]:
+                    copy.wait()
             block = x[l, dz].astype(F32)
             square = jnp.sum(block * block, axis=1, keepdims=True)
             scaled = (block * gains[pl.ds(l, 1), columns(dz)]).astype(BF16)
@@ -169,13 +196,19 @@
                 scaled, w_in[l, :, columns(dz)], (((1,), (1,)), ((), ())),
                 preferred_element_type=F32,
             )
-            if i == 0:
+            if dz == 0:
                 sacc[...] = square
                 acc[...] = sums
             else:
                 sacc[...] += square
                 acc[...] += sums
 
+        for dz in range(n_tp):
+            pass_on(dz)
+            if dz > 0:
+                complete(dz - 1)
+        complete(n_tp - 1)
+
         @pl.when(l == 0)
         def _():
             for copy in mask_copies:
@@ -183,8 +216,10 @@
 
         inverse = lax.rsqrt(sacc[...] / (width * n_tp) + norm_eps)
         logits = acc[:, 2 * held :] * inverse
-        hit = mask[l][:, :experts].astype(F32) > 0.5
-        logits = jnp.where(hit, logits, -jnp.inf)
+        hit = mask[:, :experts].astype(F32)
+        for n in range(1, layers):
+            hit = jnp.where(l == n, mask[:, n * experts : (n + 1) * experts].astype(F32), hit)
+        logits = jnp.where(hit > 0.5, logits, -jnp.inf)
         grown = jnp.exp(logits - jnp.max(logits, axis=1, keepdims=True))
         gates = grown / jnp.sum(grown, axis=1, keepdims=True)
         expert = lax.broadcasted_iota(jnp.int32, gates.shape, 1)
@@ -221,39 +256,55 @@
             total = own[dz] + pair_in[dz].astype(F32)
             own[dz] = total
             plane_out[dz] = total.astype(BF16)
-            for k in range(1, chips):
-                there = (-k) % chips
-                go(remote(
-                    plane_out.at[dz, at_rows(chip(k)), :], plane_in.at[l, dz, there],
-                    plane_send.at[l, dz, k], plane_recv.at[l, dz, there], plane_dev(k),
-                ))
+            if relay:
+                go(plane_copy(dz, chip(3), 3, 2))
+                go(plane_copy(dz, chip(2), 2, 2))
+            else:
+                for k in near:
+                    go(plane_copy(dz, chip(k), k, k))
+
+        def plane_copy(dz, place, slot, k):
+            return remote(
+                plane_out.at[dz, at_rows(place), :], plane_in.at[l, dz, slot],
+                plane_send.at[l, dz, slot], plane_recv.at[l, dz, slot], plane_dev(k),
+            )
+
+        def plane_landed(dz, slot):
+            landed(
+                plane_in.at[l, dz, slot], plane_send.at[l, dz, slot], plane_recv.at[l, dz, slot]
+            )
+            return plane_in[l, dz, slot].astype(F32)
+
+        def add_on(dz):
+            if relay:
+                both = own[dz, at_rows(chip(1)), :] + plane_landed(dz, 3)
+                plane_out[dz, at_rows(chip(1)), :] = both.astype(BF16)
+                go(plane_copy(dz, chip(1), 1, 1))
 
         def gather(dz):
             total = own[dz, at_rows(q), :]
-            for k in range(1, chips):
-                landed(
-                    plane_in.at[l, dz, k], plane_send.at[l, dz, k], plane_recv.at[l, dz, k]
-                )
-                total = total + plane_in[l, dz, k].astype(F32)
+            for k in near:
+                total = total + plane_landed(dz, k)
+            if dz != 0:
+                line_out[l, dz] = total.astype(BF16)
+                go(remote(
+                    line_out.at[l, dz], line_in.at[l, dz],
+                    line_send.at[l, dz], line_recv.at[l, dz], line_dev(dz),
+                ))
             return total
 
-        back = order[::-1]
+        back = list(range(n_tp))[::-1]
         for i, dz in enumerate(back):
             project(dz)
             if i > 0:
                 spread(back[i - 1])
         spread(back[-1])
-        moe = None
-        for dz in back:
-            moe = gather(dz)
-            if dz != 0:
-                there = (-dz) % n_tp
-                line_out[l, dz] = moe.astype(BF16)
-                go(remote(
-                    line_out.at[l, dz], line_in.at[l, there],
-                    line_send.at[l, dz], line_recv.at[l, there], line_dev(dz),
-                ))
-        for k in order[1:]:
+        for i, dz in enumerate(back):
+            add_on(dz)
+            if i > 0:
+                gather(back[i - 1])
+        moe = gather(back[-1])
+        for k in back[:-1]:
             landed(line_in.at[l, k], line_send.at[l, k], line_recv.at[l, k])
             moe = moe + line_in[l, k].astype(F32)
         hidden = (x[l, 0, at_rows(q), :].astype(F32) + moe).astype(BF16)
@@ -283,7 +334,7 @@
     vmem = pl.BlockSpec(memory_space=pltpu.VMEM)
     hbm = pl.BlockSpec(memory_space=pl.ANY)
     dma = pltpu.SemaphoreType.DMA
-    lanes = -(-experts // LANES) * LANES
+    lanes = -(-layers * experts // LANES) * LANES
     return pl.pallas_call(
         functools.partial(kernel, n_ep, n_tp, layers),
         out_shape=jax.ShapeDtypeStruct((rows, width), BF16),
@@ -291,7 +342,7 @@
         out_specs=vmem,
         scratch_shapes=[
             pltpu.VMEM((layers, n_tp, every, width), BF16),
-            pltpu.VMEM((layers, every, lanes), BF16),
+            pltpu.VMEM((every, lanes), BF16),
             pltpu.VMEM((layers, 2 * held + experts, full), BF16),
             pltpu.VMEM((layers, held, full), BF16),
             pltpu.VMEM((every, 2 * held + experts), F32),

time: 82.5 us -> 81.2 us (0.984)
  Pallas kernels: 80.9 us -> 79.5 us
    pallas_call x1, Pallas kernels: 80.9 us -> 79.5 us  [body(): pl.pallas_call(functools.partial(kernel, n_ep, n_tp, layers), out_shape=j...]
where the time goes in v2:
time: 81.2 us; the launch traced here: 81 us
  Pallas kernels  79.5 us (98%)
  local copies, waits for them, and re-layouts  1.47 us (2%)
    pallas_call x1, Pallas kernels, body(): pl.pallas_call(functools.partial(kernel, n_ep, n_tp, layers), out_shape=j...  79.5 us

profile of v2, /device:TPU:0, one launch (start us, length us, event | category | flops | bytes accessed | tf_op | source)
XLA Modules:
  0.0 81.0 jit_solution(14394034523957439905)
XLA Ops:
  0.0 79.5 %shard_map.73 = bf16[32,1024]{1,0:T(8,128)(2,1)} custom-call(bf16[32,1024]{1,0:T(8,128)(2,1)} %tokens.1, f32[2,4096]{1,0:T(2,128)} %gains.1, bf16[2,16,4096]{2,1,0:T(8,128)(2,1)} %bitcast.8, bf16[2,2,192,4096]{3,2,1,0:T(8,128)(2,1)} %bitcast.5, bf16[2,2,192,4096]{3,2,1,0:T(8,128)(2,1)} %bitcast.6, bf16[2,384,4096]{2,1,0:T(8,128)(2,1)} %bitcast.7, ...), custom_call_target="tpu_custom_call" | custom-call | tf_op jit(solution)/shard_map/pallas_call | solution.py:338
  79.5 1.5 %copy.9 = bf16[32,1024]{1,0:T(8,128)(2,1)} copy(bf16[32,1024]{1,0:T(8,128)(2,1)} %shard_map.73) | data formatting | bytes 131072

commit v3 on v2

v3 whole, which is shorter than its diff:
```python
import functools

import jax
import jax.numpy as jnp
from jax import lax
from jax.experimental import pallas as pl
from jax.experimental.pallas import tpu as pltpu
from jax.sharding import PartitionSpec as P

MESH = pl.DeviceIdType.MESH
BF16, F32 = jnp.bfloat16, jnp.float32
CORES = 2
LANES = 128
PIECES = 1

norm_eps = 1e-06


def flip(index, k):
    bit = 1
    while bit <= k:
        if k & bit:
            index = index + bit * (1 - 2 * lax.rem(lax.div(index, bit), 2))
        bit *= 2
    return index


def kernel(
    n_ep, n_tp, layers, pieces,
    tokens, gains, router, w_gate, w_up, w_down, ids,
    out,
    x, mask, w_in, wd, acc, sacc, inner, own, pair_out, pair_in, plane_out, plane_in,
    line_out, line_in,
    w_sem, mask_send, mask_recv, x_send, x_recv, pair_send, pair_recv, plane_send, plane_recv,
    line_send, line_recv,
):
    rows, width = tokens.shape[0], tokens.shape[1] // pieces
    chips = n_ep // CORES
    half = chips * rows
    local_exp, hidden_units = w_gate.shape[1:3]
    experts, top = router.shape[1], ids.shape[1]
    held = local_exp * hidden_units
    me, z = lax.axis_index("ep"), lax.axis_index("tp")
    q, c = lax.div(me, CORES), lax.rem(me, CORES)
    sibling = (q * CORES + 1 - c, z)

    relay = chips == 4

    chip_at = [[flip(q, k) for k in range(chips)] for _ in range(2)]
    if relay:
        for odd, at in enumerate(chip_at):
            turn = lax.rem(c + odd, 2) * (at[2] - at[1])
            at[1:3] = [at[1] + turn, at[2] - turn]
    plane_at = [[(i * CORES + c, z) for i in at] for at in chip_at]
    line_at = [(me, flip(z, k)) for k in range(n_tp)]
    first_column = [at * (pieces * width) for _, at in line_at]
    first_row = [[i * rows for i in at] for at in chip_at]

    def row_range(k, base=0, dz=0):
        return pl.ds(pl.multiple_of(base + first_row[dz % 2][k], rows), rows)

    chunks = n_tp * pieces

    def columns(j):
        start = first_column[j // pieces] + j % pieces * width
        return pl.ds(pl.multiple_of(start, width), width)

    def weight_copies(l):
        pairs = [(router.at[l], w_in.at[l, pl.ds(2 * held, experts), :])]
        for i, source in enumerate((w_gate, w_up)):
            for e in range(local_exp):
                place = pl.ds(i * held + e * hidden_units, hidden_units)
                pairs.append((source.at[l, e], w_in.at[l, place, :]))
        pairs.append((w_down.at[l], wd.at[l]))
        return [
            pltpu.make_async_copy(src, dst, w_sem.at[l, i]) for i, (src, dst) in enumerate(pairs)
        ]

    for l in range(layers):
        for copy in weight_copies(l):
            copy.start()

    barrier = pltpu.get_barrier_semaphore()
    for k in range(1, n_ep):
        pl.semaphore_signal(
            barrier, inc=1, device_id=(lax.rem(me + k, n_ep), z), device_id_type=MESH
        )
    for k in range(1, n_tp):
        pl.semaphore_signal(barrier, inc=1, device_id=line_at[k], device_id_type=MESH)

    for p in range(pieces):
        x[0, p, row_range(0), :] = tokens[:, p * width : (p + 1) * width]
    lane = lax.broadcasted_iota(jnp.int32, (rows, mask.shape[1]), 1)
    hit = None
    for l in range(layers):
        chosen = ids[l].T + l * experts
        for k in range(top):
            named = chosen[:, k : k + 1] == lane
            hit = named if hit is None else hit | named
    mask[row_range(0), :] = jnp.where(hit, 1.0, 0.0).astype(BF16)

    pl.semaphore_wait(barrier, n_ep - 1 + n_tp - 1)

    def remote(src, dst, send, recv, device):
        return pltpu.make_async_remote_copy(
            src_ref=src, dst_ref=dst, send_sem=send, recv_sem=recv,
            device_id=device, device_id_type=MESH,
        )

    mask_copies = []
    for k in range(1, n_ep):
        mask_copies.append(
            remote(
                mask.at[row_range(0), :],
                mask.at[row_range(0, (k % CORES) * half), :],
                mask_send.at[k], mask_recv.at[k],
                (lax.rem(me + k, n_ep), z),
            )
        )

    def layer(l, carry):
        sends = []

        def go(copy):
            copy.start()
            sends.append(copy)

        def to_line(j):
            return remote(
                x.at[l, j % pieces, row_range(0), :], x.at[l, j, row_range(0), :],
                x_send.at[l, 0, j, 0], x_recv.at[l, 0, j, q], line_at[j // pieces],
            )

        def to_plane(dz, k):
            ref = x.at[l, dz, row_range(0), :]
            return remote(
                ref, ref, x_send.at[l, 1, dz, k], x_recv.at[l, 0, dz, q], plane_at[dz % 2][k]
            )

        def onward(dz):
            ref = x.at[l, dz, row_range(1, 0, dz), :]
            return remote(
                ref, ref, x_send.at[l, 1, dz, 3], x_recv.at[l, 0, dz, chip_at[dz % 2][1]], plane_at[dz % 2][2]
            )

        def to_sibling(dz):
            return remote(
                x.at[l, dz, pl.ds(0, half), :], x.at[l, dz, pl.ds(half, half), :],
                x_send.at[l, 2, dz, 0], x_recv.at[l, 1, dz, 0], sibling,
            )

        def arrive(parity, dz, k):
            ref = x.at[l, dz, row_range(k, parity * half, dz), :]
            pltpu.make_async_remote_copy(
                src_ref=ref, dst_ref=ref, send_sem=x_send.at[l, 0, 0, 0],
                recv_sem=x_recv.at[l, parity, dz, chip_at[dz % 2][k]],
                device_id=sibling, device_id_type=MESH,
            ).wait_recv()

        near = range(1, 3 if relay else chips)
        for j in range(pieces, chunks):
            go(to_line(j))
        for j in range(pieces):
            for k in near:
                go(to_plane(j, k))

        @pl.when(l == 0)
        def _():
            for copy in mask_copies:
                copy.start()

        def pass_on(dz):
            ahead = dz + pieces
            if ahead < chunks:
                arrive(0, ahead, 0)
                for k in near:
                    go(to_plane(ahead, k))
            for k in near:
                arrive(0, dz, k)
                if relay and k == 1:
                    go(onward(dz))

        def complete(dz):
            if relay:
                arrive(0, dz, 3)
            both = to_sibling(dz)
            go(both)
            both.wait_recv()
            if dz == 0:
                for copy in weight_copies(l)[:-1]:
                    copy.wait()
            block = x[l, dz].astype(F32)
            square = jnp.sum(block * block, axis=1, keepdims=True)
            scaled = (block * gains[pl.ds(l, 1), columns(dz)]).astype(BF16)
            sums = lax.dot_general(
                scaled, w_in[l, :, columns(dz)], (((1,), (1,)), ((), ())),
                preferred_element_type=F32,
            )
            if dz == 0:
                sacc[...] = square
                acc[...] = sums
            else:
                sacc[...] += square
                acc[...] += sums

        for dz in range(chunks):
            pass_on(dz)
            if dz > 0:
                complete(dz - 1)
        complete(chunks - 1)

        @pl.when(l == 0)
        def _():
            for copy in mask_copies:
                copy.wait_recv()

        inverse = lax.rsqrt(sacc[...] / (width * chunks) + norm_eps)
        logits = acc[:, 2 * held :] * inverse
        hit = mask[:, :experts].astype(F32)
        for n in range(1, layers):
            hit = jnp.where(l == n, mask[:, n * experts : (n + 1) * experts].astype(F32), hit)
        logits = jnp.where(hit > 0.5, logits, -jnp.inf)
        grown = jnp.exp(logits - jnp.max(logits, axis=1, keepdims=True))
        gates = grown / jnp.sum(grown, axis=1, keepdims=True)
        expert = lax.broadcasted_iota(jnp.int32, gates.shape, 1)
        unit = lax.broadcasted_iota(jnp.int32, (1, held), 1)
        weight = None
        for e in range(local_exp):
            gate = jnp.sum(
                jnp.where(expert == me * local_exp + e, gates, 0.0), axis=1, keepdims=True
            )
            weight = gate if e == 0 else jnp.where(unit < e * hidden_units, weight, gate)
        v = acc[:, :held] * inverse
        u = acc[:, held : 2 * held] * inverse
        inner[...] = (v / (1.0 + jnp.exp(-v)) * u * weight).astype(BF16)

        weight_copies(l)[-1].wait()

        def project(dz):
            total = jnp.dot(inner[...], wd[l, :, columns(dz)], preferred_element_type=F32)
            pair_out[dz] = total[half:].astype(BF16)
            own[dz] = total[:half]
            go(remote(
                pair_out.at[dz], pair_in.at[dz],
                pair_send.at[l, dz], pair_recv.at[l, dz], sibling,
            ))

        def landed(ref, send, recv):
            pltpu.make_async_remote_copy(
                src_ref=ref, dst_ref=ref, send_sem=send, recv_sem=recv,
                device_id=sibling, device_id_type=MESH,
            ).wait_recv()

        def spread(dz):
            landed(pair_in.at[dz], pair_send.at[l, dz], pair_recv.at[l, dz])
            total = own[dz] + pair_in[dz].astype(F32)
            own[dz] = total
            plane_out[dz] = total.astype(BF16)
            if relay:
                go(plane_copy(dz, 3, 3, 2))
                go(plane_copy(dz, 2, 2, 2))
            else:
                for k in near:
                    go(plane_copy(dz, k, k, k))

        def plane_copy(dz, place, slot, k):
            return remote(
                plane_out.at[dz, row_range(place, 0, dz), :], plane_in.at[l, dz, slot],
                plane_send.at[l, dz, slot], plane_recv.at[l, dz, slot], plane_at[dz % 2][k],
            )

        def plane_landed(dz, slot):
            landed(
                plane_in.at[l, dz, slot], plane_send.at[l, dz, slot], plane_recv.at[l, dz, slot]
            )
            return plane_in[l, dz, slot].astype(F32)

        def add_on(dz):
            if relay:
                both = own[dz, row_range(1, 0, dz), :] + plane_landed(dz, 3)
                plane_out[dz, row_range(1, 0, dz), :] = both.astype(BF16)
                go(plane_copy(dz, 1, 1, 1))

        def gather(dz):
            total = own[dz, row_range(0), :]
            for k in near:
                total = total + plane_landed(dz, k)
            if dz >= pieces:
                line_out[l, dz] = total.astype(BF16)
                go(remote(
                    line_out.at[l, dz], line_in.at[l, dz],
                    line_send.at[l, dz], line_recv.at[l, dz], line_at[dz // pieces],
                ))
            return total

        back = [d * pieces + p for d in reversed(range(n_tp)) for p in range(pieces)]
        for i, dz in enumerate(back):
            project(dz)
            if i > 0:
                spread(back[i - 1])
        spread(back[-1])
        moe = {}
        for i, dz in enumerate(back):
            add_on(dz)
            if i > 0:
                moe[back[i - 1]] = gather(back[i - 1])
        moe[back[-1]] = gather(back[-1])
        hidden = []
        for p in range(pieces):
            total = moe[p]
            for d in reversed(range(1, n_tp)):
                k = d * pieces + p
                landed(line_in.at[l, k], line_send.at[l, k], line_recv.at[l, k])
                total = total + line_in[l, k].astype(F32)
            hidden.append((x[l, p, row_range(0), :].astype(F32) + total).astype(BF16))
        for copy in sends:
            copy.wait_send()
        for p in range(pieces):
            out[:, p * width : (p + 1) * width] = hidden[p]

        @pl.when(l < layers - 1)
        def _():
            for p in range(pieces):
                x[lax.rem(l + 1, layers), p, row_range(0), :] = hidden[p]

        return carry

    lax.fori_loop(0, layers, layer, 0)
    for copy in mask_copies:
        copy.wait_send()


def body(tokens, norm_gains, router, w_gate, w_up, w_down, expert_ids):
    n_ep, n_tp = lax.axis_size("ep"), lax.axis_size("tp")
    layers, local_exp, full, hidden = w_gate.shape
    experts = router.shape[2]
    held = local_exp * hidden
    chips = n_ep // CORES
    pieces = PIECES if chips == 4 else 1
    rows, width = tokens.shape[0], tokens.shape[1] // pieces
    chunks = n_tp * pieces
    every, half = n_ep * rows, chips * rows
    vmem = pl.BlockSpec(memory_space=pltpu.VMEM)
    hbm = pl.BlockSpec(memory_space=pl.ANY)
    dma = pltpu.SemaphoreType.DMA
    lanes = -(-layers * experts // LANES) * LANES
    return pl.pallas_call(
        functools.partial(kernel, n_ep, n_tp, layers, pieces),
        out_shape=jax.ShapeDtypeStruct(tokens.shape, BF16),
        in_specs=[vmem, vmem, vmem, hbm, hbm, hbm, vmem],
        out_specs=vmem,
        scratch_shapes=[
            pltpu.VMEM((layers, chunks, every, width), BF16),
            pltpu.VMEM((every, lanes), BF16),
            pltpu.VMEM((layers, 2 * held + experts, full), BF16),
            pltpu.VMEM((layers, held, full), BF16),
            pltpu.VMEM((every, 2 * held + experts), F32),
            pltpu.VMEM((every, 1), F32),
            pltpu.VMEM((every, held), BF16),
            pltpu.VMEM((chunks, half, width), F32),
            pltpu.VMEM((chunks, half, width), BF16),
            pltpu.VMEM((chunks, half, width), BF16),
            pltpu.VMEM((chunks, half, width), BF16),
            pltpu.VMEM((layers, chunks, chips, rows, width), BF16),
            pltpu.VMEM((layers, chunks, rows, width), BF16),
            pltpu.VMEM((layers, chunks, rows, width), BF16),
            dma((layers, 2 + 2 * local_exp)),
            dma((n_ep,)),
            dma((n_ep,)),
            dma((layers, 3, chunks, chips)),
            dma((layers, 2, chunks, chips)),
            dma((layers, chunks)),
            dma((layers, chunks)),
            dma((layers, chunks, chips)),
            dma((layers, chunks, chips)),
            dma((layers, chunks)),
            dma((layers, chunks)),
        ],
        compiler_params=pltpu.CompilerParams(
            collective_id=0, has_side_effects=True, vmem_limit_bytes=67043328
        ),
    )(
        tokens, norm_gains, router.swapaxes(1, 2), w_gate.swapaxes(2, 3), w_up.swapaxes(2, 3),
        w_down.reshape(layers, held, full), expert_ids.swapaxes(1, 2),
    )


def solution(mesh):
    in_specs = (
        P("ep", "tp"),
        P(),
        P(),
        P(None, "ep", None, "tp"),
        P(None, "ep", None, "tp"),
        P(None, "ep", "tp", None),
        P(None, "ep", None),
    )
    return jax.shard_map(
        body, mesh=mesh, in_specs=in_specs, out_specs=P("ep", "tp"), check_vma=False
    )
```

time: 81.2 us -> 88.2 us (1.086)
  Pallas kernels: 79.5 us -> 86.5 us
    pallas_call x1, Pallas kernels: 79.5 us -> 86.5 us  [body(): pl.pallas_call(functools.partial(kernel, n_ep, n_tp, layers, pieces), out...]
where the time goes in v3:
time: 88.2 us; the launch traced here: 88 us
  Pallas kernels  86.5 us (98%)
  local copies, waits for them, and re-layouts  1.47 us (2%)
    pallas_call x1, Pallas kernels, body(): pl.pallas_call(functools.partial(kernel, n_ep, n_tp, layers, pieces), out...  86.5 us

profile of v3, /device:TPU:0, one launch (start us, length us, event | category | flops | bytes accessed | tf_op | source)
XLA Modules:
  0.0 88.0 jit_solution(11267536185497188130)
XLA Ops:
  0.0 86.5 %shard_map.73 = bf16[32,1024]{1,0:T(8,128)(2,1)} custom-call(bf16[32,1024]{1,0:T(8,128)(2,1)} %tokens.1, f32[2,4096]{1,0:T(2,128)} %gains.1, bf16[2,16,4096]{2,1,0:T(8,128)(2,1)} %bitcast.8, bf16[2,2,192,4096]{3,2,1,0:T(8,128)(2,1)} %bitcast.5, bf16[2,2,192,4096]{3,2,1,0:T(8,128)(2,1)} %bitcast.6, bf16[2,384,4096]{2,1,0:T(8,128)(2,1)} %bitcast.7, ...), custom_call_target="tpu_custom_call" | custom-call | tf_op jit(solution)/shard_map/pallas_call | solution.py:347
  86.5 1.5 %copy.9 = bf16[32,1024]{1,0:T(8,128)(2,1)} copy(bf16[32,1024]{1,0:T(8,128)(2,1)} %shard_map.73) | data formatting | bytes 131072
